TPU v7x, 32 devices: a whole 2x2x4 slice. The times are simulated.
32 devices in a mesh: crop: 2 (over x), seq: 2 (over y), res: 8 (over z, core).
Axes of the slice: x: 2, y: 2, z: 4, core: 2. Of those that a mesh axis runs over, the one named last changes fastest.
Arguments:
- aligned_chain_embedding: bfloat16 [128, 32, 256], P(('crop', 'seq'), 'res'), parts along dimension 0, may hold values from -6 to 6
- alignment_mask: int32 [128, 32], P(('crop', 'seq'), 'res'), parts along dimension 0, may hold values from 0 to 1, as said below
- resolved_residue_mask: int32 [64], P('crop'), parts along dimension 0, may hold values 0 or 1
- pairwise_state: bfloat16 [64, 32, 128], P(('crop', 'seq'), 'res'), parts along dimension 0, may hold values from -8 to 8
- combined_projection_matrix: bfloat16 [256, 1024], replicated, may hold values from -0.375 to 0.375
- pair_bias_weight: bfloat16 [128, 8], replicated, may hold values from -8 to 8
- final_projection_matrix: bfloat16 [256, 256], replicated, may hold values from -0.375 to 0.375
- left_right_projection_matrix: bfloat16 [256, 64], replicated, may hold values from -1.5 to 1.5
- outer_mean_weight: bfloat16 [1024, 128], replicated, may hold values from -0.1875 to 0.1875
Outputs:
- alignment_output: bfloat16 [128, 32, 256], P(('crop', 'seq'), 'res'), parts along dimension 0
- pairwise_output: bfloat16 [64, 32, 128], P(('crop', 'seq'), 'res'), parts along dimension 0
There are 2 independent parts, one for each index of `crop`. A program takes and returns all parts, laid end to end along the dimension named above; an argument that names none is the same for every part. Nothing has to cross between parts.
Inputs may be any that keep to these rules, and one draw needn't show every extreme that they name: `alignment_mask`: sequence 0 has no gaps.
All inputs are finite; a program needn't handle non-finite values.
Results may differ from a plain program's by a relative error of at most 0.013.
The roundings to bfloat16 on the way count: a program that leaves them out, or rounds other values in their place, can miss the bound.
Values may be sent and summed in bfloat16 or wider, within the bound.
A program may use at most 64 MiB of HBM per device.

v0:
```python
import math

import jax
import jax.numpy as jnp
from jax import lax
from jax.sharding import PartitionSpec as P

ROW_FEATURES = 256
CZ = 128
HEAD_NUMBER = 8
PER_HEAD_DIM = 32
PROJ_FEATURES = 32


epsilon = 1e-05


def layer_normalize(values):
    values = values.astype(jnp.float32)
    average = jnp.mean(values, axis=-1, keepdims=True)
    centered = values - average
    variance = jnp.mean(centered * centered, axis=-1, keepdims=True)
    return centered * lax.rsqrt(variance + epsilon)


def outer_rows(left_side, right_side, project):
    row_total = left_side.shape[1]
    col_total = right_side.shape[1]
    block_rows = math.gcd(row_total, max(1, 2048 // col_total))

    def outer_block(start):
        product = jnp.einsum(
            "sic,sje->ijce", left_side, right_side, preferred_element_type=jnp.float32
        )
        flattened = product.reshape(block_rows * col_total, PROJ_FEATURES * PROJ_FEATURES)
        return jnp.dot(flattened, project, precision=lax.Precision.HIGHEST).reshape(
            block_rows, col_total, CZ
        )

    starts = jnp.arange(row_total // block_rows, dtype=jnp.int32) * block_rows
    return lax.map(outer_block, starts).reshape(row_total, col_total, CZ)


def per_device(
    aligned_chain_embedding,
    alignment_mask,
    resolved_residue_mask,
    pairwise_state,
    combined_projection_matrix,
    pair_bias_weight,
    final_projection_matrix,
    left_right_projection_matrix,
    outer_mean_weight,
):
    chain_count = aligned_chain_embedding.shape[0]
    amino_count = aligned_chain_embedding.shape[1]
    res_ranks = lax.axis_size("res")
    seq_groups = lax.axis_size("seq")
    full_length = amino_count * res_ranks
    row_count = full_length // seq_groups
    item_count = HEAD_NUMBER * chain_count // res_ranks
    per_head = min(item_count, chain_count)
    head_count = item_count // per_head
    my_rank = lax.axis_index("res")
    my_group = lax.axis_index("seq")
    standardized_rows = layer_normalize(aligned_chain_embedding).astype(jnp.bfloat16)
    linear_mapped = jnp.dot(
        standardized_rows.reshape(chain_count * amino_count, ROW_FEATURES),
        combined_projection_matrix,
        preferred_element_type=jnp.float32,
    )
    linear_mapped = linear_mapped.reshape(chain_count, amino_count, 4, HEAD_NUMBER, PER_HEAD_DIM)
    queries = (linear_mapped[:, :, 0] * PER_HEAD_DIM ** (-0.5)).astype(jnp.bfloat16)
    key_rows = linear_mapped[:, :, 1].astype(jnp.bfloat16)
    value_rows = linear_mapped[:, :, 2].astype(jnp.bfloat16)
    sigmoid_factor = jax.nn.sigmoid(linear_mapped[:, :, 3])
    stacked = jnp.stack([queries, key_rows, value_rows], axis=2)
    stacked = jnp.transpose(stacked, (3, 0, 1, 2, 4)).reshape(
        HEAD_NUMBER * chain_count, amino_count, 3 * PER_HEAD_DIM
    )
    presence_mask_flags = alignment_mask.astype(jnp.bfloat16)
    key_flags = jnp.broadcast_to(
        presence_mask_flags[None], (HEAD_NUMBER, chain_count, amino_count)
    ).reshape(HEAD_NUMBER * chain_count, amino_count)
    arrived, arrived_flags = (
        lax.all_to_all(stacked, "res", split_axis=0, concat_axis=1, tiled=True),
        lax.all_to_all(key_flags, "res", split_axis=0, concat_axis=1, tiled=True),
    )
    pair_normed = layer_normalize(pairwise_state).astype(jnp.bfloat16)
    local_bias = jnp.dot(
        pair_normed.reshape(row_count * amino_count, CZ),
        pair_bias_weight,
        preferred_element_type=jnp.float32,
    )
    local_bias = jnp.transpose(
        local_bias.astype(jnp.bfloat16).reshape(row_count, amino_count, HEAD_NUMBER), (2, 0, 1)
    )
    bias_cols = lax.all_gather(local_bias, "res", axis=2, tiled=True)
    whole_bias = lax.all_gather(bias_cols, "seq", axis=1, tiled=True)
    first_head = my_rank * item_count // chain_count
    head_bias = lax.dynamic_slice_in_dim(whole_bias, first_head, head_count, 0)
    grouped = arrived.reshape(head_count, per_head, full_length, 3, PER_HEAD_DIM)
    key_validity_mask = (
        arrived_flags.reshape(head_count, per_head, full_length).astype(jnp.float32) - 1.0
    ) * 1000000000.0
    scores = jnp.einsum(
        "gpid,gpjd->gpij",
        grouped[:, :, :, 0],
        grouped[:, :, :, 1],
        preferred_element_type=jnp.float32,
    )
    scores = scores + head_bias.astype(jnp.float32)[:, None] + key_validity_mask[:, :, None, :]
    row_max = jnp.max(scores, axis=-1, keepdims=True)
    exponent = jnp.exp(scores - row_max)
    weights = (exponent / jnp.sum(exponent, axis=-1, keepdims=True)).astype(jnp.bfloat16)
    softmax_mixed = jnp.einsum(
        "gpij,gpjd->gpid", weights, grouped[:, :, :, 2], preferred_element_type=jnp.float32
    )
    softmax_mixed = softmax_mixed.astype(jnp.bfloat16).reshape(
        item_count, full_length, PER_HEAD_DIM
    )
    returned = lax.all_to_all(softmax_mixed, "res", split_axis=1, concat_axis=0, tiled=True)
    returned = jnp.transpose(
        returned.reshape(HEAD_NUMBER, chain_count, amino_count, PER_HEAD_DIM), (1, 2, 0, 3)
    )
    sigmoid_scaled = (
        (sigmoid_factor * returned.astype(jnp.float32))
        .astype(jnp.bfloat16)
        .reshape(chain_count * amino_count, ROW_FEATURES)
    )
    embedding_increment = jnp.dot(
        sigmoid_scaled, final_projection_matrix, preferred_element_type=jnp.float32
    ).reshape(chain_count, amino_count, ROW_FEATURES)
    alignment_output = (aligned_chain_embedding.astype(jnp.float32) + embedding_increment).astype(
        jnp.bfloat16
    )
    standardized_product = layer_normalize(alignment_output).astype(jnp.bfloat16)
    left_right_vectors = jnp.dot(
        standardized_product.reshape(chain_count * amino_count, ROW_FEATURES),
        left_right_projection_matrix,
        preferred_element_type=jnp.float32,
    )
    left_right_vectors = left_right_vectors.reshape(chain_count, amino_count, 2, PROJ_FEATURES)
    entry_present = alignment_mask.astype(jnp.float32)[:, :, None]
    left_side = (left_right_vectors[:, :, 0] * entry_present).astype(jnp.bfloat16)
    right_side = (left_right_vectors[:, :, 1] * entry_present).astype(jnp.bfloat16)
    left_all, left_flags = (
        lax.all_gather(left_side, "res", axis=1, tiled=True),
        lax.all_gather(presence_mask_flags, "res", axis=1, tiled=True),
    )
    project = outer_mean_weight.astype(jnp.float32)
    row_start = my_group * row_count
    left_full, flag_full = (
        lax.all_to_all(left_all, "seq", split_axis=1, concat_axis=0, tiled=True),
        lax.all_to_all(left_flags, "seq", split_axis=1, concat_axis=0, tiled=True),
    )
    right_full, right_flags = (
        lax.all_gather(right_side, "seq", axis=0, tiled=True),
        lax.all_gather(presence_mask_flags, "seq", axis=0, tiled=True),
    )
    counts = jnp.dot(flag_full.T, right_flags, preferred_element_type=jnp.float32)
    outer = outer_rows(left_full, right_full, project)
    col_start = my_rank * amino_count
    row_mask = lax.dynamic_slice_in_dim(resolved_residue_mask, row_start, row_count).astype(
        jnp.float32
    )
    col_mask = lax.dynamic_slice_in_dim(resolved_residue_mask, col_start, amino_count).astype(
        jnp.float32
    )
    pair_mask = row_mask[:, None] * col_mask[None, :]
    pairwise_output = (
        pairwise_state.astype(jnp.float32) + pair_mask[:, :, None] * (outer / counts[:, :, None])
    ).astype(jnp.bfloat16)
    return (alignment_output, pairwise_output)


def solution(mesh):
    placed = (
        P(("crop", "seq"), "res", None),
        P(("crop", "seq"), "res"),
        P("crop"),
        P(("crop", "seq"), "res", None),
        P(),
        P(),
        P(),
        P(),
        P(),
    )
    return jax.shard_map(
        per_device,
        mesh=mesh,
        in_specs=placed,
        out_specs=(P(("crop", "seq"), "res", None), P(("crop", "seq"), "res", None)),
        check_vma=False,
    )
```

profile of v0, /device:TPU:0, one launch (start us, length us, event | category | flops | bytes accessed | tf_op | source)
XLA Modules:
  0.0 115.8 jit_solution(7931450124926292603)
XLA Ops:
  0.6 0.8 fusion.49
  1.4 13.5 %all-gather = bf16[8,4,32]{2,1,0:T(4,128)(2,1)S(1)} all-gather(bf16[1,4,32]{2,1,0:T(4,128)(2,1)S(1)} %bitcast.150), channel_id=1, replica_groups=mesh['crop'=2,'seq'=2,'res'=8] {'res'}, dimensions={0}, use_global_device_ids=true | all-gather | bytes 2304 | tf_op jit(solution)/shard_map/all_gather | solution.py:149
  14.9 0.7 reshape.211
  15.5 3.2 %all-to-all-start.4 = ((bf16[2,2,256]{2,1,0:T(2,128)(2,1)}), bf16[2,2,256]{2,1,0:T(2,128)(2,1)S(1)}, u32[]{:S(2)}, u32[]{:S(2)}) async-start(bf16[2,2,256]{2,1,0:T(2,128)(2,1)} %reshape.211), calls=%async_computation.4 | async-start | bytes 4096 | tf_op jit(solution)/shard_map/all_to_all | solution.py:155
  18.8 1.2 %copy.71 = bf16[256,1024]{0,1:T(8,128)(2,1)S(1)} copy(bf16[256,1024]{1,0:T(8,128)(2,1)} %param.13) | data formatting | bytes 1048576 | tf_op args[4]
  20.0 0.9 convert_reduce_fusion
  21.0 1.0 fusion.21
  22.0 1.4 %fusion.30 = f32[32,4,4,8,32]{4,0,3,2,1:T(8,128)S(1)} fusion(bf16[4,8,32,256,1]{3,2,1,0,4:T(8,128)(2,1)S(1)} %bitcast.138, f32[32,4]{0,1:T(4,128)S(1)} %add_rsqrt_fusion.2, f32[32,4]{0,1:T(4,128)S(1)} %broadcast_multiply_fusion.3, bf16[32,4,256]{2,1,0:T(4,128)(2,1)} %param.9), kind=kOutput, calls=%fused_computation.47 | convolution fusion | flops 67239936 | bytes 1115136 | tf_op jit(solution)/shard_map/dot_general | solution.py:67
  23.4 0.1 slice.74
  23.6 0.1 convert_reduce_fusion.2
  23.7 0.2 fusion.44
  23.9 0.1 fusion.45
  24.0 0.1 convolution_convert_fusion.1
  24.1 0.1 copy.80
  24.3 0.1 copy.81
  24.3 14.0 %all_gather.18 = bf16[8,16,32]{1,0,2:T(8,128)(2,1)S(1)} all-gather(bf16[8,16,4]{1,0,2:T(8,128)(2,1)S(1)} %copy.81), channel_id=1, replica_groups=mesh['crop'=2,'seq'=2,'res'=8] {'res'}, dimensions={2}, use_global_device_ids=true | all-gather | bytes 9216 | tf_op jit(solution)/shard_map/all_gather | solution.py:98
  38.3 0.1 copy.82
  38.5 4.6 %all_gather.19 = bf16[8,32,32]{2,0,1:T(8,128)(2,1)S(1)} all-gather(bf16[8,16,32]{2,0,1:T(8,128)(2,1)S(1)} %copy.82), channel_id=1, replica_groups=mesh['crop'=2,'seq'=2,'res'=8] {'seq'}, dimensions={1}, use_global_device_ids=true | all-gather | bytes 24576 | tf_op jit(solution)/shard_map/all_gather | solution.py:99
  43.1 1.0 maximum_bitcast_fusion
  44.1 0.1 dynamic-slice_convert_fusion
  44.2 0.6 broadcast_in_dim.4
  44.8 3.3 %all-to-all-start.1 = ((bf16[8,32,4]{1,2,0:T(4,128)(2,1)}), bf16[8,32,4]{1,2,0:T(4,128)(2,1)S(1)}, u32[]{:S(2)}, u32[]{:S(2)}) async-start(bf16[8,32,4]{1,2,0:T(4,128)(2,1)} %broadcast_in_dim.4), calls=%async_computation.1 | async-start | bytes 16384 | tf_op jit(solution)/shard_map/all_to_all | solution.py:87
  48.1 0.1 dynamic-slice_convert_fusion.1
  48.2 1.8 %copy.103 = bf16[8,32,4,3,32]{4,3,2,1,0:T(4,128)(2,1)S(1)} copy(bf16[8,32,4,3,32]{4,1,0,3,2:T(8,128)(2,1)} %maximum_bitcast_fusion) | data formatting | bytes 393216 | tf_op jit(solution)/shard_map/reshape | solution.py:78
  50.0 1.2 %reshape.205 = bf16[256,4,96]{2,1,0:T(4,128)(2,1)} reshape(bf16[8,32,4,3,32]{4,3,2,1,0:T(4,128)(2,1)S(1)} %copy.103) | data formatting | bytes 393216 | tf_op jit(solution)/shard_map/reshape | solution.py:78
  51.3 4.2 %all-gather.1 = bf16[2,32,4]{1,2,0:T(4,128)(2,1)S(1)} all-gather(bf16[1,32,4]{1,2,0:T(4,128)(2,1)S(1)} %bitcast.151), channel_id=1, replica_groups=mesh['crop'=2,'seq'=2,'res'=8] {'seq'}, dimensions={0}, use_global_device_ids=true | all-gather | bytes 768 | tf_op jit(solution)/shard_map/all_gather | solution.py:159
  55.5 0.1 reshape.196
  55.6 5.0 %all-to-all-start = ((bf16[256,4,96]{2,1,0:T(4,128)(2,1)}), bf16[256,4,96]{2,1,0:T(4,128)(2,1)S(1)}, u32[]{:S(2)}, u32[]{:S(2)}) async-start(bf16[256,4,96]{2,1,0:T(4,128)(2,1)} %reshape.205), calls=%async_computation | async-start | bytes 524288 | tf_op jit(solution)/shard_map/all_to_all | solution.py:86
  60.7 0.1 reshape.212
  60.8 0.1 copy.85
  60.9 9.5 %all-to-all-done = bf16[256,4,96]{2,1,0:T(4,128)(2,1)S(1)} async-done(((bf16[256,4,96]{2,1,0:T(4,128)(2,1)}), bf16[256,4,96]{2,1,0:T(4,128)(2,1)S(1)}, u32[]{:S(2)}, u32[]{:S(2)}) %all-to-all-start) | async-done | bytes 196640 | tf_op jit(solution)/shard_map/all_to_all | solution.py:86
  70.4 0.7 copy.75
  71.1 2.2 %reshape.185 = bf16[1,32,32,3,32]{4,3,1,2,0:T(4,128)(2,1)S(1)} reshape(bf16[32,8,4,96]{3,0,2,1:T(8,128)(2,1)} %copy.75) | data formatting | bytes 393216 | tf_op jit(solution)/shard_map/reshape | solution.py:102
  73.3 2.0 %fusion.48 = (bf16[1,32,32,1,32]{4,3,1,2,0:T(2,128)(2,1)S(1)}, bf16[1,32,32,1,32]{4,3,1,2,0:T(2,128)(2,1)S(1)}, bf16[1,32,32,1,32]{4,3,1,2,0:T(2,128)(2,1)}) fusion(bf16[1,32,32,3,32]{4,3,1,2,0:T(4,128)(2,1)S(1)} %reshape.185), kind=kLoop, calls=%fused_computation.80 | loop fusion | bytes 393216 | tf_op jit(solution)/shard_map/slice | solution.py:108
  75.3 0.7 fusion.3
  76.0 0.2 fusion.50
  76.2 1.5 %convolution_convert_fusion = bf16[32,32,32]{2,1,0:T(8,128)(2,1)S(1)} fusion(bf16[1,32,32,1,32]{4,3,1,2,0:T(2,128)(2,1)} %get-tuple-element.27, f32[32,32]{1,0:T(8,128)S(1)} %fusion.50, f32[32,32,32]{1,2,0:T(8,128)S(1)} %fusion.3), kind=kOutput, calls=%fused_computation.6 | convolution fusion | flops 2229279 | bytes 266240 | tf_op jit(solution)/shard_map/gpij,gpjd->gpid/dot_general | solution.py:116
  77.8 0.1 copy.136
  77.9 0.9 reshape.207
  78.8 3.4 %all-to-all-start.2 = ((bf16[8,2,2048]{2,1,0:T(2,128)(2,1)}), bf16[8,2,2048]{2,1,0:T(2,128)(2,1)S(1)}, u32[]{:S(2)}, u32[]{:S(2)}) async-start(bf16[8,2,2048]{2,1,0:T(2,128)(2,1)} %reshape.207), calls=%async_computation.2 | async-start | bytes 131072 | tf_op jit(solution)/shard_map/all_to_all | solution.py:122
  82.2 0.1 all_to_all.65
  82.2 5.7 %all-to-all-done.2 = bf16[8,2,2048]{2,1,0:T(2,128)(2,1)S(1)} async-done(((bf16[8,2,2048]{2,1,0:T(2,128)(2,1)}), bf16[8,2,2048]{2,1,0:T(2,128)(2,1)S(1)}, u32[]{:S(2)}, u32[]{:S(2)}) %all-to-all-start.2) | async-done | bytes 65568 | tf_op jit(solution)/shard_map/all_to_all | solution.py:122
  88.0 0.2 reshape.208
  88.2 0.1 fusion.14
  88.3 0.1 copy.90
  88.4 0.2 dot_general.47
  88.6 0.2 convert_reduce_fusion.1
  88.9 0.2 fusion.23
  89.1 0.2 fusion.27
  89.3 0.1 fusion.35
  89.4 14.2 %all_gather.21 = bf16[32,32,32]{2,0,1:T(8,128)(2,1)S(1)} all-gather(bf16[32,4,32]{2,0,1:T(8,128)(2,1)S(1)} %get-tuple-element.29), channel_id=1, replica_groups=mesh['crop'=2,'seq'=2,'res'=8] {'res'}, dimensions={1}, use_global_device_ids=true | all-gather | bytes 73728 | tf_op jit(solution)/shard_map/all_gather | solution.py:148
  103.6 0.9 reshape.209
  104.5 3.3 %all-to-all-start.3 = ((bf16[2,2,8192]{2,1,0:T(2,128)(2,1)}), bf16[2,2,8192]{2,1,0:T(2,128)(2,1)S(1)}, u32[]{:S(2)}, u32[]{:S(2)}) async-start(bf16[2,2,8192]{2,1,0:T(2,128)(2,1)} %reshape.209), calls=%async_computation.3 | async-start | bytes 131072 | tf_op jit(solution)/shard_map/all_to_all | solution.py:154
  107.8 0.1 fusion.51
  107.9 0.7 copy.97
  108.6 4.6 %all_gather.20 = bf16[64,4,32]{2,0,1:T(8,128)(2,1)S(1)} all-gather(bf16[32,4,32]{2,0,1:T(8,128)(2,1)S(1)} %get-tuple-element.28), channel_id=1, replica_groups=mesh['crop'=2,'seq'=2,'res'=8] {'seq'}, dimensions={0}, use_global_device_ids=true | all-gather | bytes 24576 | tf_op jit(solution)/shard_map/all_gather | solution.py:158
  113.2 0.2 reshape.210
  113.4 0.2 copy.92
  113.6 0.1 reshape.203
  113.7 0.4 convolution_bitcast_fusion
  114.1 0.3 copy.94
  114.4 0.5 dot_general.53
  114.9 0.3 fusion.7
  115.2 0.6 copy.98
  (34 shorter events, 0.4 us)
Async XLA Ops:
  0.6 114.3 %copy-start = (bf16[1024,128]{1,0:T(8,128)(2,1)S(1)}, bf16[1024,128]{1,0:T(8,128)(2,1)}, u32[]{:S(2)}) copy-start(bf16[1024,128]{1,0:T(8,128)(2,1)} %param.17) | copy-start | bytes 786436
  15.5 28.7 %all-to-all-start.4 = ((bf16[2,2,256]{2,1,0:T(2,128)(2,1)}), bf16[2,2,256]{2,1,0:T(2,128)(2,1)S(1)}, u32[]{:S(2)}, u32[]{:S(2)}) async-start(bf16[2,2,256]{2,1,0:T(2,128)(2,1)} %reshape.211), calls=%async_computation.4 | async-start | bytes 4096 | tf_op jit(solution)/shard_map/all_to_all | solution.py:155
  22.0 1.6 %copy-start.2 = (bf16[16,4,128]{2,1,0:T(4,128)(2,1)S(1)}, bf16[16,4,128]{2,1,0:T(4,128)(2,1)}, u32[]{:S(2)}) copy-start(bf16[16,4,128]{2,1,0:T(4,128)(2,1)} %param.12) | copy-start | bytes 49156
  22.0 2.0 %copy-start.5 = (bf16[128,8]{0,1:T(8,128)(2,1)S(1)}, bf16[128,8]{0,1:T(8,128)(2,1)}, u32[]{:S(2)}) copy-start(bf16[128,8]{0,1:T(8,128)(2,1)} %param.14) | copy-start | bytes 6148
  23.4 20.7 %copy-start.6 = (s32[32]{0:T(128)S(1)}, s32[32]{0:T(128)}, u32[]{:S(2)}) copy-start(s32[32]{0:T(128)} %param.11) | copy-start | bytes 388
  44.8 10.8 %all-to-all-start.1 = ((bf16[8,32,4]{1,2,0:T(4,128)(2,1)}), bf16[8,32,4]{1,2,0:T(4,128)(2,1)S(1)}, u32[]{:S(2)}, u32[]{:S(2)}) async-start(bf16[8,32,4]{1,2,0:T(4,128)(2,1)} %broadcast_in_dim.4), calls=%async_computation.1 | async-start | bytes 16384 | tf_op jit(solution)/shard_map/all_to_all | solution.py:87
  55.6 14.7 %all-to-all-start = ((bf16[256,4,96]{2,1,0:T(4,128)(2,1)}), bf16[256,4,96]{2,1,0:T(4,128)(2,1)S(1)}, u32[]{:S(2)}, u32[]{:S(2)}) async-start(bf16[256,4,96]{2,1,0:T(4,128)(2,1)} %reshape.205), calls=%async_computation | async-start | bytes 524288 | tf_op jit(solution)/shard_map/all_to_all | solution.py:86
  77.7 10.9 %copy-start.1 = (bf16[32,4,256]{2,1,0:T(4,128)(2,1)S(1)}, bf16[32,4,256]{2,1,0:T(4,128)(2,1)}, u32[]{:S(2)}) copy-start(bf16[32,4,256]{2,1,0:T(4,128)(2,1)} %param.9) | copy-start | bytes 196612
  77.7 10.9 %copy-start.3 = (bf16[256,256]{1,0:T(8,128)(2,1)S(1)}, bf16[256,256]{1,0:T(8,128)(2,1)}, u32[]{:S(2)}) copy-start(bf16[256,256]{1,0:T(8,128)(2,1)} %param.15) | copy-start | bytes 393220
  77.7 11.4 %copy-start.4 = (bf16[256,64]{0,1:T(8,128)(2,1)S(1)}, bf16[256,64]{0,1:T(8,128)(2,1)}, u32[]{:S(2)}) copy-start(bf16[256,64]{0,1:T(8,128)(2,1)} %param.16) | copy-start | bytes 98308
  78.8 9.2 %all-to-all-start.2 = ((bf16[8,2,2048]{2,1,0:T(2,128)(2,1)}), bf16[8,2,2048]{2,1,0:T(2,128)(2,1)S(1)}, u32[]{:S(2)}, u32[]{:S(2)}) async-start(bf16[8,2,2048]{2,1,0:T(2,128)(2,1)} %reshape.207), calls=%async_computation.2 | async-start | bytes 131072 | tf_op jit(solution)/shard_map/all_to_all | solution.py:122
  104.5 8.7 %all-to-all-start.3 = ((bf16[2,2,8192]{2,1,0:T(2,128)(2,1)}), bf16[2,2,8192]{2,1,0:T(2,128)(2,1)S(1)}, u32[]{:S(2)}, u32[]{:S(2)}) async-start(bf16[2,2,8192]{2,1,0:T(2,128)(2,1)} %reshape.209), calls=%async_computation.3 | async-start | bytes 131072 | tf_op jit(solution)/shard_map/all_to_all | solution.py:154
where the time goes:
time: 117 us; the launch traced here: 116 us
  blocking collectives  55 us (47%)
  starting transfers between devices  18.2 us (16%)
  local copies, waits for them, and re-layouts  16.4 us (14%)
  waiting for transfers between devices  15.2 us (13%)
  matrix products  4.99 us (4%)
  other arithmetic  4.97 us (4%)
    all_gather x1, blocking collectives, per_device(): lax.all_gather(left_side, 'res', axis=1, tiled=True)  14.2 us
    all_gather x1, blocking collectives, per_device(): bias_cols = lax.all_gather(local_bias, 'res', axis=2, tiled=True)  14 us
    all_gather x1, blocking collectives, per_device(): lax.all_gather(presence_mask_flags, 'res', axis=1, tiled=True)  13.5 us
    all_to_all x1, waiting for transfers between devices, per_device(): lax.all_to_all(stacked, 'res', split_axis=0, concat_axis=1, tiled=True)  9.47 us
    all_to_all x1, waiting for transfers between devices, per_device(): lax.all_to_all(softmax_mixed, 'res', split_axis=1, concat_axis=0, tiled=T...  5.73 us
    unnamed x24, local copies, waits for them, and re-layouts  5.6 us
    all_to_all x1, starting transfers between devices, per_device(): lax.all_to_all(stacked, 'res', split_axis=0, concat_axis=1, tiled=True)  5.02 us
    all_gather x1, blocking collectives, per_device(): whole_bias = lax.all_gather(bias_cols, 'seq', axis=1, tiled=True)  4.58 us
  transfers between devices with their start and end apart: 5, of which 2 were waited for; matrix products, arithmetic and copies ran while one was open for 9% of the time, Pallas kernels for 0%

commit v1 on v0

--- a/solution.py
+++ b/solution.py
@@ -1,8 +1,11 @@
+import functools
 import math
 
 import jax
 import jax.numpy as jnp
 from jax import lax
+from jax.experimental import pallas as pl
+from jax.experimental.pallas import tpu as pltpu
 from jax.sharding import PartitionSpec as P
 
 ROW_FEATURES = 256
@@ -174,6 +177,298 @@
     return (alignment_output, pairwise_output)
 
 
+LANES = 128
+F32 = jnp.float32
+BF16 = jnp.bfloat16
+
+
+def iota(shape, axis):
+    return lax.broadcasted_iota(jnp.int32, shape, axis)
+
+
+def dot(a, b, ca=1, cb=0):
+    return lax.dot_general(a, b, (((ca,), (cb,)), ((), ())), preferred_element_type=F32)
+
+
+def one_hot(cond):
+    return jnp.where(cond, 1.0, 0.0).astype(BF16)
+
+
+def fused_kernel(
+    groups, ranks, chains, aminos,
+    emb_ref, mask_ref, resolved_ref, pair_ref, proj_ref, bias_w_ref, final_ref, lr_ref, outer_ref,
+    out_ref, pair_out_ref,
+    emb_buf, aux_buf, left_send, left_buf, right_send, right_buf, out_send, out_buf,
+    weight_buf, product_buf, lhs_buf,
+    emb_s, emb_r, aux_s, aux_r, left_s, left_r, right_s, right_r, out_s, out_r,
+):
+    devices = groups * ranks
+    per = chains // ranks
+    tile = per * aminos
+    rows = ranks * tile
+    full = ranks * aminos
+    pair_rows = full // groups
+    pairs = pair_rows * aminos
+    half = rows // groups
+    group = lax.axis_index("seq")
+    rank = lax.axis_index("res")
+    me = group * ranks + rank
+
+    def peer_of(k):
+        peer = lax.rem(me + k, devices)
+        return peer, {"seq": peer // ranks, "res": lax.rem(peer, ranks)}
+
+    barrier = pltpu.get_barrier_semaphore()
+    for k in range(1, devices):
+        pl.semaphore_signal(
+            barrier, inc=1, device_id=peer_of(k)[1], device_id_type=pl.DeviceIdType.MESH
+        )
+
+    def send(src, dst, ssem, rsem, device):
+        copy = pltpu.make_async_remote_copy(
+            src_ref=src, dst_ref=dst, send_sem=ssem, recv_sem=rsem,
+            device_id=device, device_id_type=pl.DeviceIdType.MESH,
+        )
+        copy.start()
+        return copy
+
+    pair_value = pair_ref[...]
+    pair_normed = layer_normalize(pair_value).astype(BF16)
+    wide = jnp.concatenate([pair_normed] * groups, axis=0)
+    wide = jnp.where(iota((groups * pairs, CZ), 0) // pairs == group, wide, jnp.zeros_like(wide))
+    own_bias = dot(bias_w_ref[...], wide, 0, 1)
+    spread = dot(mask_ref[...].astype(F32).astype(BF16), one_hot(
+        iota((aminos, LANES), 1) % aminos == iota((aminos, LANES), 0)))
+    flag_row = jnp.sum(
+        jnp.where(iota((chains, LANES), 1) // aminos == iota((chains, LANES), 0), spread, 0.0),
+        axis=0, keepdims=True)
+    flags = jnp.broadcast_to(flag_row, (HEAD_NUMBER, LANES))
+    aux_buf[me] = jnp.concatenate([own_bias, flags], axis=0).astype(BF16)
+    emb_buf[rank] = emb_ref[rank]
+
+    pl.semaphore_wait(barrier, devices - 1)
+    pending = []
+    emb_copies = []
+    for k in range(1, ranks):
+        peer = lax.rem(rank + k, ranks)
+        emb_copies.append(send(emb_ref.at[peer], emb_buf.at[rank], emb_s.at[k], emb_r.at[k],
+                               {"seq": group, "res": peer}))
+    aux_copies = []
+    for k in range(1, devices):
+        aux_copies.append(send(aux_buf.at[me], aux_buf.at[me], aux_s.at[k], aux_r.at[k],
+                               peer_of(k)[1]))
+
+    per_c = aminos * PROJ_FEATURES
+    for c in range(PROJ_FEATURES):
+        piece = outer_ref[c * PROJ_FEATURES:(c + 1) * PROJ_FEATURES, :]
+        for j in range(aminos):
+            at = c * per_c + j * PROJ_FEATURES
+            weight_buf[at:at + PROJ_FEATURES, :] = piece
+    q0 = iota((pairs, pairs), 0)
+    q1 = iota((pairs, pairs), 1)
+    order = one_hot((q0 % pair_rows) * aminos + q0 // pair_rows == q1)
+    pair_turned = dot(order, pair_value)
+    lane_r = iota((pairs, full), 1)
+    row_r = iota((pairs, full), 0)
+    resolved = jnp.broadcast_to(resolved_ref[...].astype(F32), (pairs, full))
+    pair_mask = jnp.sum(
+        jnp.where(lane_r == group * pair_rows + row_r % pair_rows, resolved, 0.0),
+        axis=1, keepdims=True
+    ) * jnp.sum(
+        jnp.where(lane_r == rank * aminos + row_r // pair_rows, resolved, 0.0),
+        axis=1, keepdims=True)
+
+    for copy in emb_copies:
+        copy.wait_recv()
+    embedding = emb_buf[...].reshape(rows, ROW_FEATURES)
+    normed = layer_normalize(embedding).astype(BF16)
+    projected = dot(normed, proj_ref[...])
+    width = HEAD_NUMBER * PER_HEAD_DIM
+    queries = (projected[:, :width] * PER_HEAD_DIM ** (-0.5)).astype(BF16)
+    keys = projected[:, width:2 * width].astype(BF16)
+    values = projected[:, 2 * width:3 * width].astype(BF16)
+    gating = jax.nn.sigmoid(projected[:, 3 * width:])
+
+    for copy in aux_copies:
+        copy.wait_recv()
+    aux = aux_buf[...].astype(F32)
+    bias_all = aux[0:ranks, :HEAD_NUMBER]
+    for g in range(1, groups):
+        bias_all = bias_all + aux[g * ranks:(g + 1) * ranks, :HEAD_NUMBER]
+    bias_all = bias_all.reshape(ranks * HEAD_NUMBER, LANES).astype(BF16)
+    hq = (HEAD_NUMBER * rows, ranks * HEAD_NUMBER)
+    pick = one_hot(
+        ((iota(hq, 0) % rows) // tile) * HEAD_NUMBER + iota(hq, 0) // rows == iota(hq, 1))
+    bias_q = dot(pick, bias_all)
+    hl = (HEAD_NUMBER * rows, LANES)
+    bias_q = jnp.where(iota(hl, 1) % aminos == iota(hl, 0) % aminos, bias_q, 0.0).astype(BF16)
+    pp = iota((rows, LANES), 0)
+    ll = iota((rows, LANES), 1)
+    row_pick = one_hot(ll // aminos == (pp // tile) * aminos + pp % aminos)
+    bias_full = dot(row_pick, bias_q, 1, 1)
+    flag_all = aux[:, HEAD_NUMBER:HEAD_NUMBER + 1].reshape(devices, LANES).astype(BF16)
+    near = dot(flag_all, one_hot(pp == rank * tile + ll % tile))
+    near_row = jnp.sum(
+        jnp.where(
+            iota((devices, LANES), 0) == group * ranks + iota((devices, LANES), 1) // tile,
+            near, 0.0),
+        axis=0, keepdims=True)
+    key_mask = (near_row - 1.0) * 1000000000.0
+    present = jnp.sum(jnp.where(pp == ll, near_row, 0.0), axis=1, keepdims=True)
+    same_chain = (pp // aminos) % per == (ll // aminos) % per
+    heads_per = LANES // PER_HEAD_DIM
+    mixed = []
+    for block in range(width // LANES):
+        cols = slice(block * LANES, (block + 1) * LANES)
+        total = jnp.zeros((rows, LANES), F32)
+        for sub in range(heads_per):
+            head = block * heads_per + sub
+            lanes = ll // PER_HEAD_DIM == sub
+            query = jnp.where(lanes, queries[:, cols], jnp.zeros((), BF16))
+            scores = dot(query, keys[:, cols], 1, 1)
+            scores = scores + bias_full[:, head * rows:(head + 1) * rows] + key_mask
+            scores = jnp.where(same_chain, scores, -3e38)
+            exponent = jnp.exp(scores - jnp.max(scores, axis=1, keepdims=True))
+            weights = (exponent / jnp.sum(exponent, axis=1, keepdims=True)).astype(BF16)
+            total = jnp.where(lanes, dot(weights, values[:, cols]), total)
+        mixed.append(total)
+    attended = jnp.concatenate(mixed, axis=1).astype(BF16)
+    gated = (gating * attended.astype(F32)).astype(BF16)
+    updated = (embedding.astype(F32) + dot(gated, final_ref[...])).astype(BF16)
+    normed_out = layer_normalize(updated).astype(BF16)
+
+    folds = LANES // half
+    low = PROJ_FEATURES // folds
+    left_t = dot(lr_ref[:, :PROJ_FEATURES], normed_out, 0, 1) * near_row
+    for g in range(groups):
+        part = left_t[:, g * half:(g + 1) * half]
+        left_send[g] = jnp.concatenate(
+            [part[f * low:(f + 1) * low] for f in range(folds)], axis=1).astype(BF16)
+    right_w = jnp.concatenate([lr_ref[:, PROJ_FEATURES:]] * aminos, axis=1)
+    right = dot(normed_out, right_w) * present
+    right = jnp.where(ll // PROJ_FEATURES == pp % aminos, right, 0.0).astype(BF16)
+    right_send[...] = right.reshape(ranks, tile, LANES)
+    out_send[...] = updated.reshape(ranks, tile, ROW_FEATURES)
+    left_copies = []
+    for k in range(1, devices):
+        peer, device = peer_of(k)
+        left_copies.append(send(left_send.at[peer // ranks], left_buf.at[me],
+                                left_s.at[k], left_r.at[k], device))
+        left_copies.append(send(right_send.at[lax.rem(peer, ranks)], right_buf.at[me],
+                                right_s.at[k], right_r.at[k], device))
+    out_copies = []
+    for k in range(1, ranks):
+        peer = lax.rem(rank + k, ranks)
+        out_copies.append(send(out_send.at[peer], out_buf.at[rank], out_s.at[k], out_r.at[k],
+                               {"seq": group, "res": peer}))
+    left_buf[me] = left_send[group]
+    right_buf[me] = right_send[rank]
+    out_buf[rank] = out_send[rank]
+
+    gq = (groups * pairs, devices)
+    gl = (groups * pairs, LANES)
+    within = iota(gl, 0) % pairs
+    row_at = group * pair_rows + within % pair_rows
+    group_q = iota(gq, 0) // pairs
+    row_at_q = group * pair_rows + (iota(gq, 0) % pairs) % pair_rows
+    row_flags = dot(one_hot(group_q * ranks + row_at_q // aminos == iota(gq, 1)), flag_all)
+    col_flags = dot(one_hot(group_q * ranks + rank == iota(gq, 1)), flag_all)
+    amino_l = iota(gl, 1) % aminos
+    gather_s = one_hot(pp // aminos == ll)
+    row_flags = dot(one_hot((amino_l == row_at % aminos) & (row_flags > 0.5)), gather_s)
+    col_flags = dot(one_hot((amino_l == within // pair_rows) & (col_flags > 0.5)), gather_s)
+    both = jnp.sum(row_flags * col_flags, axis=1, keepdims=True)
+    counts = both[:pairs]
+    for g in range(1, groups):
+        counts = counts + both[g * pairs:(g + 1) * pairs]
+
+    rep = one_hot(
+        (iota((LANES, tile), 0) // aminos) % per == iota((LANES, tile), 1) // aminos)
+    il = (folds * pair_rows, 1, LANES)
+    lane = iota(il, 2)
+    lead = iota(il, 0)
+    place = lane % half
+    keep = (lane // half == lead % folds) & (
+        (place // tile) * aminos + place % aminos == lead // folds)
+    keep = jnp.where(keep, 1.0, 0.0)
+    keep = jnp.broadcast_to(keep, (folds * pair_rows, low, LANES)).reshape(
+        pair_rows * PROJ_FEATURES, LANES).astype(BF16).reshape(folds * pair_rows, low, LANES)
+
+    for copy in left_copies:
+        copy.wait_recv()
+    product = jnp.zeros((pair_rows * PROJ_FEATURES, LANES), F32)
+    for k in range(devices):
+        right_k = dot(rep, right_buf[k]).astype(BF16)
+        left_k = (left_buf[k][None] * keep).reshape(pair_rows * PROJ_FEATURES, LANES)
+        product = product + dot(left_k, right_k)
+    product_buf[...] = product
+    for c in range(PROJ_FEATURES):
+        slab = product_buf[pl.ds(c, pair_rows, stride=PROJ_FEATURES), :]
+        lanes = iota((pair_rows, LANES), 1) // PROJ_FEATURES
+        for j in range(aminos):
+            lhs_buf[j * pair_rows:(j + 1) * pair_rows, c * per_c:(c + 1) * per_c] = jnp.where(
+                lanes == j, slab, 0.0).astype(BF16)
+    outer = dot(lhs_buf[...], weight_buf[...])
+    result = (pair_turned + pair_mask * (outer / counts)).astype(BF16)
+    pair_out_ref[...] = dot(order, result, 0, 0).astype(BF16)
+
+    for copy in out_copies:
+        copy.wait_recv()
+    out_ref[...] = out_buf[...]
+    for copy in emb_copies + aux_copies + left_copies + out_copies:
+        copy.wait_send()
+
+
+def fused(*args):
+    emb, mask, resolved, pair = args[:4]
+    groups, ranks = lax.axis_size("seq"), lax.axis_size("res")
+    chains, aminos = emb.shape[:2]
+    tile = chains // ranks * aminos
+    pair_rows = pair.shape[0]
+    devices = groups * ranks
+    vmem = pl.BlockSpec(memory_space=pltpu.VMEM)
+    dma = pltpu.SemaphoreType.DMA
+    out, pair_out = pl.pallas_call(
+        functools.partial(fused_kernel, groups, ranks, chains, aminos),
+        out_shape=(
+            jax.ShapeDtypeStruct((ranks, tile, ROW_FEATURES), BF16),
+            jax.ShapeDtypeStruct((pair_rows * aminos, CZ), BF16),
+        ),
+        in_specs=[vmem] * 9,
+        out_specs=(vmem, vmem),
+        scratch_shapes=[
+            pltpu.VMEM((ranks, tile, ROW_FEATURES), BF16),
+            pltpu.VMEM((devices, 2 * HEAD_NUMBER, LANES), BF16),
+            pltpu.VMEM((groups, tile, LANES), BF16),
+            pltpu.VMEM((devices, tile, LANES), BF16),
+            pltpu.VMEM((ranks, tile, LANES), BF16),
+            pltpu.VMEM((devices, tile, LANES), BF16),
+            pltpu.VMEM((ranks, tile, ROW_FEATURES), BF16),
+            pltpu.VMEM((ranks, tile, ROW_FEATURES), BF16),
+            pltpu.VMEM((PROJ_FEATURES * LANES, CZ), BF16),
+            pltpu.VMEM((pair_rows * PROJ_FEATURES, LANES), F32),
+            pltpu.VMEM((pair_rows * aminos, PROJ_FEATURES * LANES), BF16),
+            dma((ranks,)), dma((ranks,)), dma((devices,)), dma((devices,)),
+            dma((devices,)), dma((devices,)), dma((devices,)), dma((devices,)),
+            dma((ranks,)), dma((ranks,)),
+        ],
+        compiler_params=pltpu.CompilerParams(collective_id=0, has_side_effects=True),
+    )(
+        emb.reshape(ranks, tile, ROW_FEATURES), mask, resolved.reshape(1, -1),
+        pair.reshape(-1, CZ), *args[4:],
+    )
+    return out.reshape(emb.shape), pair_out.reshape(pair.shape)
+
+
+def fits(mesh, emb, pair):
+    groups, ranks = mesh.shape["seq"], mesh.shape["res"]
+    chains, aminos = emb.shape[:2]
+    if chains % ranks or aminos * PROJ_FEATURES != LANES or chains * aminos != LANES:
+        return False
+    pairs = pair.shape[0] * aminos
+    return pairs * groups == LANES and chains // ranks * aminos * groups == PROJ_FEATURES
+
+
 def solution(mesh):
     placed = (
         P(("crop", "seq"), "res", None),
@@ -186,8 +481,11 @@
         P(),
         P(),
     )
+    def either(*args):
+        return (fused if fits(mesh, args[0], args[3]) else per_device)(*args)
+
     return jax.shard_map(
-        per_device,
+        either,
         mesh=mesh,
         in_specs=placed,
         out_specs=(P(("crop", "seq"), "res", None), P(("crop", "seq"), "res", None)),

time: 117 us -> 32.1 us (0.27)
  blocking collectives: 55 us -> 0 us
  Pallas kernels: 0 us -> 24.6 us
  starting transfers between devices: 18.2 us -> 0 us
  waiting for transfers between devices: 15.2 us -> 0 us
  local copies, waits for them, and re-layouts: 16.4 us -> 6.41 us
  matrix products: 4.99 us -> 0 us
  other arithmetic: 4.97 us -> 0 us
    all_gather x6 -> x0, blocking collectives: 55 us -> none  [the longest x1 14.2 us: per_device(): lax.all_gather(left_side, 'res', axis=1, tiled=True)]
    pallas_call x0 -> x1, Pallas kernels: none -> 24.6 us  [fused(): pl.pallas_call(functools.partial(fused_kernel, groups, ranks, chains, ami...]
    all_to_all x5 -> x0, starting transfers between devices: 18.2 us -> none  [the longest x1 5.02 us: per_device(): lax.all_to_all(stacked, 'res', split_axis=0, concat_axis=1, tiled=True)]
    all_to_all x5 -> x0, waiting for transfers between devices: 15.2 us -> none  [the longest x1 9.47 us: per_device(): lax.all_to_all(stacked, 'res', split_axis=0, concat_axis=1, tiled=True)]
    dot_general x9 -> x0, matrix products: 4.99 us -> none  [the longest x1 1.55 us: per_device(): jnp.einsum('gpij,gpjd->gpid', weights, grouped[:, :, :, 2], preferred_ele...]
    reduce_sum x5 -> x0, other arithmetic: 2.35 us -> none  [the longest x3 1.33 us: layer_normalize(): variance = jnp.mean(centered * centered, axis=-1, keepdims=True)]
    reshape x3 -> x2, local copies, waits for them, and re-layouts: 5.2 us -> 2.99 us  [the longest x1 1.49 us: fused(): emb.reshape(ranks, tile, ROW_FEATURES)]
    unnamed x24 -> x12, local copies, waits for them, and re-layouts: 5.6 us -> 3.43 us
  transfers between devices with their start and end apart: 5 -> 0, of which waited for: 2 -> 0; matrix products, arithmetic and copies ran while one was open for 9% -> 0% of each run, Pallas kernels for 0% -> 0%
where the time goes in v1:
time: 32.1 us; the launch traced here: 31.7 us
  Pallas kernels  24.6 us (77%)
  local copies, waits for them, and re-layouts  6.41 us (20%)
  between operations  0.66 us (2%)
    pallas_call x1, Pallas kernels, fused(): pl.pallas_call(functools.partial(fused_kernel, groups, ranks, chains, ami...  24.6 us
    unnamed x12, local copies, waits for them, and re-layouts  3.43 us
    reshape x1, local copies, waits for them, and re-layouts, fused(): emb.reshape(ranks, tile, ROW_FEATURES)  1.49 us
    reshape x1, local copies, waits for them, and re-layouts, fused(): return (out.reshape(emb.shape), pair_out.reshape(pair.shape))  1.49 us

profile of v1, /device:TPU:0, one launch (start us, length us, event | category | flops | bytes accessed | tf_op | source)
XLA Modules:
  0.0 31.7 jit_solution(5617030588547472541)
XLA Ops:
  0.6 0.0 copy-start.2
  0.6 0.7 %copy-done.2 = s32[32,4]{0,1:T(4,128)S(1)} copy-done((s32[32,4]{0,1:T(4,128)S(1)}, s32[32,4]{0,1:T(4,128)}, u32[]{:S(2)}) %copy-start.2) | copy-done | bytes 536
  1.3 0.0 copy-start.3
  1.3 0.7 %copy.11.mask_ref = s32[32,4]{1,0:T(8,128)} copy(s32[32,4]{0,1:T(4,128)S(1)} %copy-done.2) | data formatting | bytes 1024 | tf_op args[1]
  2.0 0.0 copy-done.3
  2.0 0.7 %copy.12.bias_w_ref = bf16[128,8]{1,0:T(8,128)(2,1)} copy(bf16[128,8]{0,1:T(8,128)(2,1)S(1)} %copy-done.3) | data formatting | bytes 4096 | tf_op args[5]
  2.7 0.0 copy-start
  2.7 1.5 %reshape.19.emb_ref = bf16[8,16,256]{2,1,0:T(8,128)(2,1)} reshape(bf16[32,4,256]{2,1,0:T(4,128)(2,1)} %param.9) | data formatting | bytes 131072 | tf_op jit(solution)/shard_map/reshape | solution.py:457
  4.2 0.0 copy-done
  4.2 0.7 %copy.13.lr_ref = bf16[256,64]{1,0:T(8,128)(2,1)} copy(bf16[256,64]{0,1:T(8,128)(2,1)S(1)} %copy-done) | data formatting | bytes 65536 | tf_op args[7]
  5.0 24.6 %shard_map.104 = (bf16[8,16,256]{2,1,0:T(8,128)(2,1)}, bf16[64,128]{1,0:T(8,128)(2,1)}) custom-call(bf16[8,16,256]{2,1,0:T(8,128)(2,1)} %reshape.19.emb_ref, s32[32,4]{1,0:T(8,128)} %copy.11.mask_ref, s32[1,32]{1,0:T(1,128)} %bitcast.5, bf16[64,128]{1,0:T(8,128)(2,1)} %bitcast.3, bf16[256,1024]{1,0:T(8,128)(2,1)} %proj_ref.1, ...), custom_call_target="tpu_custom_call" | custom-call | tf_op jit(solution)/shard_map/pallas_call | solution.py:431
  29.6 0.0 copy-start.1
  29.6 1.5 %reshape.22 = bf16[32,4,256]{2,1,0:T(4,128)(2,1)} reshape(bf16[8,16,256]{2,1,0:T(8,128)(2,1)} %get-tuple-element.4) | data formatting | bytes 131072 | tf_op jit(solution)/shard_map/reshape | solution.py:460
  31.1 0.0 copy-done.1
  31.1 0.6 %copy.15 = bf16[16,4,128]{2,1,0:T(4,128)(2,1)} copy(bf16[16,4,128]{2,1,0:T(4,128)(2,1)S(1)} %bitcast.4) | data formatting | bytes 32768
Async XLA Ops:
  0.6 0.7 %copy-start.2 = (s32[32,4]{0,1:T(4,128)S(1)}, s32[32,4]{0,1:T(4,128)}, u32[]{:S(2)}) copy-start(s32[32,4]{0,1:T(4,128)} %param.10) | copy-start | bytes 1540
  1.3 0.7 %copy-start.3 = (bf16[128,8]{0,1:T(8,128)(2,1)S(1)}, bf16[128,8]{0,1:T(8,128)(2,1)}, u32[]{:S(2)}) copy-start(bf16[128,8]{0,1:T(8,128)(2,1)} %param.14) | copy-start | bytes 6148
  2.7 1.5 %copy-start = (bf16[256,64]{0,1:T(8,128)(2,1)S(1)}, bf16[256,64]{0,1:T(8,128)(2,1)}, u32[]{:S(2)}) copy-start(bf16[256,64]{0,1:T(8,128)(2,1)} %param.16) | copy-start | bytes 98308
  29.6 1.5 %copy-start.1 = (bf16[64,128]{1,0:T(8,128)(2,1)S(1)}, bf16[64,128]{1,0:T(8,128)(2,1)}, u32[]{:S(2)}) copy-start(bf16[64,128]{1,0:T(8,128)(2,1)} %get-tuple-element.5) | copy-start | bytes 49156

commit v2 on v1

--- a/solution.py
+++ b/solution.py
@@ -199,7 +199,7 @@
     emb_ref, mask_ref, resolved_ref, pair_ref, proj_ref, bias_w_ref, final_ref, lr_ref, outer_ref,
     out_ref, pair_out_ref,
     emb_buf, aux_buf, left_send, left_buf, right_send, right_buf, out_send, out_buf,
-    weight_buf, product_buf, lhs_buf,
+    product_buf, lhs_buf,
     emb_s, emb_r, aux_s, aux_r, left_s, left_r, right_s, right_r, out_s, out_r,
 ):
     devices = groups * ranks
@@ -236,43 +236,44 @@
     pair_normed = layer_normalize(pair_value).astype(BF16)
     wide = jnp.concatenate([pair_normed] * groups, axis=0)
     wide = jnp.where(iota((groups * pairs, CZ), 0) // pairs == group, wide, jnp.zeros_like(wide))
-    own_bias = dot(bias_w_ref[...], wide, 0, 1)
+    own_bias = dot(bias_w_ref[...], wide, 1, 1)
     spread = dot(mask_ref[...].astype(F32).astype(BF16), one_hot(
-        iota((aminos, LANES), 1) % aminos == iota((aminos, LANES), 0)))
+        iota((chains, LANES), 1) // aminos == iota((chains, LANES), 0)))
     flag_row = jnp.sum(
-        jnp.where(iota((chains, LANES), 1) // aminos == iota((chains, LANES), 0), spread, 0.0),
+        jnp.where(iota((aminos, LANES), 1) % aminos == iota((aminos, LANES), 0), spread, 0.0),
         axis=0, keepdims=True)
     flags = jnp.broadcast_to(flag_row, (HEAD_NUMBER, LANES))
     aux_buf[me] = jnp.concatenate([own_bias, flags], axis=0).astype(BF16)
-    emb_buf[rank] = emb_ref[rank]
+    own = pl.ds(rank * per, per)
+    emb_buf[own] = emb_ref[own]
 
     pl.semaphore_wait(barrier, devices - 1)
     pending = []
     emb_copies = []
     for k in range(1, ranks):
         peer = lax.rem(rank + k, ranks)
-        emb_copies.append(send(emb_ref.at[peer], emb_buf.at[rank], emb_s.at[k], emb_r.at[k],
+        emb_copies.append(send(emb_ref.at[pl.ds(peer * per, per)], emb_buf.at[own],
+                               emb_s.at[k], emb_r.at[k],
                                {"seq": group, "res": peer}))
     aux_copies = []
     for k in range(1, devices):
         aux_copies.append(send(aux_buf.at[me], aux_buf.at[me], aux_s.at[k], aux_r.at[k],
                                peer_of(k)[1]))
 
-    per_c = aminos * PROJ_FEATURES
-    for c in range(PROJ_FEATURES):
-        piece = outer_ref[c * PROJ_FEATURES:(c + 1) * PROJ_FEATURES, :]
-        for j in range(aminos):
-            at = c * per_c + j * PROJ_FEATURES
-            weight_buf[at:at + PROJ_FEATURES, :] = piece
+    quads = pair_rows // aminos
+
+    def row_of(q):
+        return (q % quads) * aminos + (q % pair_rows) // quads
+
     q0 = iota((pairs, pairs), 0)
     q1 = iota((pairs, pairs), 1)
-    order = one_hot((q0 % pair_rows) * aminos + q0 // pair_rows == q1)
+    order = one_hot(row_of(q0) * aminos + q0 // pair_rows == q1)
     pair_turned = dot(order, pair_value)
     lane_r = iota((pairs, full), 1)
     row_r = iota((pairs, full), 0)
     resolved = jnp.broadcast_to(resolved_ref[...].astype(F32), (pairs, full))
     pair_mask = jnp.sum(
-        jnp.where(lane_r == group * pair_rows + row_r % pair_rows, resolved, 0.0),
+        jnp.where(lane_r == group * pair_rows + row_of(row_r), resolved, 0.0),
         axis=1, keepdims=True
     ) * jnp.sum(
         jnp.where(lane_r == rank * aminos + row_r // pair_rows, resolved, 0.0),
@@ -280,7 +281,7 @@
 
     for copy in emb_copies:
         copy.wait_recv()
-    embedding = emb_buf[...].reshape(rows, ROW_FEATURES)
+    embedding = emb_buf[...].astype(F32).reshape(rows, ROW_FEATURES)
     normed = layer_normalize(embedding).astype(BF16)
     projected = dot(normed, proj_ref[...])
     width = HEAD_NUMBER * PER_HEAD_DIM
@@ -334,21 +335,22 @@
         mixed.append(total)
     attended = jnp.concatenate(mixed, axis=1).astype(BF16)
     gated = (gating * attended.astype(F32)).astype(BF16)
-    updated = (embedding.astype(F32) + dot(gated, final_ref[...])).astype(BF16)
+    updated = (embedding + dot(gated, final_ref[...])).astype(BF16)
     normed_out = layer_normalize(updated).astype(BF16)
 
-    folds = LANES // half
-    low = PROJ_FEATURES // folds
-    left_t = dot(lr_ref[:, :PROJ_FEATURES], normed_out, 0, 1) * near_row
+    left_w = jnp.concatenate([lr_ref[:PROJ_FEATURES, :]] * quads, axis=0)
+    right_w = jnp.concatenate([lr_ref[PROJ_FEATURES:, :]] * aminos, axis=0)
+    left = dot(normed_out, left_w, 1, 1) * present
+    left = jnp.where(ll // PROJ_FEATURES == (pp // tile) % quads, left, 0.0)
     for g in range(groups):
-        part = left_t[:, g * half:(g + 1) * half]
-        left_send[g] = jnp.concatenate(
-            [part[f * low:(f + 1) * low] for f in range(folds)], axis=1).astype(BF16)
-    right_w = jnp.concatenate([lr_ref[:, PROJ_FEATURES:]] * aminos, axis=1)
-    right = dot(normed_out, right_w) * present
+        part = left[g * half:g * half + tile]
+        for r in range(1, quads):
+            part = part + left[g * half + r * tile:g * half + (r + 1) * tile]
+        left_send[g] = part.astype(BF16)
+    right = dot(normed_out, right_w, 1, 1) * present
     right = jnp.where(ll // PROJ_FEATURES == pp % aminos, right, 0.0).astype(BF16)
     right_send[...] = right.reshape(ranks, tile, LANES)
-    out_send[...] = updated.reshape(ranks, tile, ROW_FEATURES)
+    out_send[...] = updated.astype(F32).reshape(chains, aminos, ROW_FEATURES).astype(BF16)
     left_copies = []
     for k in range(1, devices):
         peer, device = peer_of(k)
@@ -359,18 +361,18 @@
     out_copies = []
     for k in range(1, ranks):
         peer = lax.rem(rank + k, ranks)
-        out_copies.append(send(out_send.at[peer], out_buf.at[rank], out_s.at[k], out_r.at[k],
+        out_copies.append(send(out_send.at[pl.ds(peer * per, per)], out_buf.at[own], out_s.at[k], out_r.at[k],
                                {"seq": group, "res": peer}))
     left_buf[me] = left_send[group]
     right_buf[me] = right_send[rank]
-    out_buf[rank] = out_send[rank]
+    out_buf[own] = out_send[own]
 
     gq = (groups * pairs, devices)
     gl = (groups * pairs, LANES)
     within = iota(gl, 0) % pairs
-    row_at = group * pair_rows + within % pair_rows
+    row_at = group * pair_rows + row_of(within)
     group_q = iota(gq, 0) // pairs
-    row_at_q = group * pair_rows + (iota(gq, 0) % pairs) % pair_rows
+    row_at_q = group * pair_rows + row_of(iota(gq, 0) % pairs)
     row_flags = dot(one_hot(group_q * ranks + row_at_q // aminos == iota(gq, 1)), flag_all)
     col_flags = dot(one_hot(group_q * ranks + rank == iota(gq, 1)), flag_all)
     amino_l = iota(gl, 1) % aminos
@@ -382,33 +384,31 @@
     for g in range(1, groups):
         counts = counts + both[g * pairs:(g + 1) * pairs]
 
-    rep = one_hot(
-        (iota((LANES, tile), 0) // aminos) % per == iota((LANES, tile), 1) // aminos)
-    il = (folds * pair_rows, 1, LANES)
-    lane = iota(il, 2)
-    lead = iota(il, 0)
-    place = lane % half
-    keep = (lane // half == lead % folds) & (
-        (place // tile) * aminos + place % aminos == lead // folds)
-    keep = jnp.where(keep, 1.0, 0.0)
-    keep = jnp.broadcast_to(keep, (folds * pair_rows, low, LANES)).reshape(
-        pair_rows * PROJ_FEATURES, LANES).astype(BF16).reshape(folds * pair_rows, low, LANES)
-
+    depth = devices * tile
+    rep = one_hot(iota((depth, depth), 0) // aminos == iota((depth, depth), 1) // aminos)
+    amino_d = iota((depth, LANES), 0) % aminos
+    block = iota((pair_rows, LANES), 1) // PROJ_FEATURES
     for copy in left_copies:
         copy.wait_recv()
-    product = jnp.zeros((pair_rows * PROJ_FEATURES, LANES), F32)
-    for k in range(devices):
-        right_k = dot(rep, right_buf[k]).astype(BF16)
-        left_k = (left_buf[k][None] * keep).reshape(pair_rows * PROJ_FEATURES, LANES)
-        product = product + dot(left_k, right_k)
-    product_buf[...] = product
-    for c in range(PROJ_FEATURES):
-        slab = product_buf[pl.ds(c, pair_rows, stride=PROJ_FEATURES), :]
-        lanes = iota((pair_rows, LANES), 1) // PROJ_FEATURES
+    left_all = left_buf[...].reshape(depth, LANES)
+    right_all = dot(rep, right_buf[...].reshape(depth, LANES))
+    right_all = jnp.concatenate(
+        [jnp.where(amino_d == a, right_all, 0.0).astype(BF16) for a in range(aminos)], axis=1)
+    product = dot(left_all, right_all, 0, 0)
+    for a in range(aminos):
+        product_buf[a * LANES:(a + 1) * LANES, :] = product[:, a * LANES:(a + 1) * LANES]
+    for c in range(0, PROJ_FEATURES, aminos):
+        slabs = [product_buf[pl.ds(c + x, pair_rows, stride=PROJ_FEATURES), :]
+                 for x in range(aminos)]
         for j in range(aminos):
-            lhs_buf[j * pair_rows:(j + 1) * pair_rows, c * per_c:(c + 1) * per_c] = jnp.where(
-                lanes == j, slab, 0.0).astype(BF16)
-    outer = dot(lhs_buf[...], weight_buf[...])
+            turned = jnp.zeros((pair_rows, LANES), F32)
+            for x in range(aminos):
+                shift = (x - j) % aminos * PROJ_FEATURES
+                moved = pltpu.roll(slabs[x], shift, 1) if shift else slabs[x]
+                turned = jnp.where(block == x, moved, turned)
+            lhs_buf[j * pair_rows:(j + 1) * pair_rows,
+                    c * PROJ_FEATURES:c * PROJ_FEATURES + LANES] = turned.astype(BF16)
+    outer = dot(lhs_buf[...], outer_ref[...])
     result = (pair_turned + pair_mask * (outer / counts)).astype(BF16)
     pair_out_ref[...] = dot(order, result, 0, 0).astype(BF16)
 
@@ -431,33 +431,32 @@
     out, pair_out = pl.pallas_call(
         functools.partial(fused_kernel, groups, ranks, chains, aminos),
         out_shape=(
-            jax.ShapeDtypeStruct((ranks, tile, ROW_FEATURES), BF16),
+            jax.ShapeDtypeStruct(emb.shape, BF16),
             jax.ShapeDtypeStruct((pair_rows * aminos, CZ), BF16),
         ),
         in_specs=[vmem] * 9,
         out_specs=(vmem, vmem),
         scratch_shapes=[
-            pltpu.VMEM((ranks, tile, ROW_FEATURES), BF16),
+            pltpu.VMEM(emb.shape, BF16),
             pltpu.VMEM((devices, 2 * HEAD_NUMBER, LANES), BF16),
             pltpu.VMEM((groups, tile, LANES), BF16),
             pltpu.VMEM((devices, tile, LANES), BF16),
             pltpu.VMEM((ranks, tile, LANES), BF16),
             pltpu.VMEM((devices, tile, LANES), BF16),
-            pltpu.VMEM((ranks, tile, ROW_FEATURES), BF16),
-            pltpu.VMEM((ranks, tile, ROW_FEATURES), BF16),
-            pltpu.VMEM((PROJ_FEATURES * LANES, CZ), BF16),
+            pltpu.VMEM(emb.shape, BF16),
+            pltpu.VMEM(emb.shape, BF16),
             pltpu.VMEM((pair_rows * PROJ_FEATURES, LANES), F32),
-            pltpu.VMEM((pair_rows * aminos, PROJ_FEATURES * LANES), BF16),
+            pltpu.VMEM((pair_rows * aminos, PROJ_FEATURES * PROJ_FEATURES), BF16),
             dma((ranks,)), dma((ranks,)), dma((devices,)), dma((devices,)),
             dma((devices,)), dma((devices,)), dma((devices,)), dma((devices,)),
             dma((ranks,)), dma((ranks,)),
         ],
         compiler_params=pltpu.CompilerParams(collective_id=0, has_side_effects=True),
     )(
-        emb.reshape(ranks, tile, ROW_FEATURES), mask, resolved.reshape(1, -1),
-        pair.reshape(-1, CZ), *args[4:],
-    )
-    return out.reshape(emb.shape), pair_out.reshape(pair.shape)
+        emb, mask.T, resolved.reshape(1, -1),
+        pair.reshape(-1, CZ), args[4], args[5].T, args[6], args[7].T, args[8],
+    )
+    return out, pair_out.reshape(pair.shape)
 
 
 def fits(mesh, emb, pair):

time: 32.1 us -> 26.4 us (0.82)
  local copies, waits for them, and re-layouts: 6.41 us -> 2.11 us
  Pallas kernels: 24.6 us -> 23.5 us
    reshape x2 -> x0, local copies, waits for them, and re-layouts: 2.99 us -> none  [the longest x1 1.49 us: fused(): emb.reshape(ranks, tile, ROW_FEATURES)]
    unnamed x12 -> x4, local copies, waits for them, and re-layouts: 3.43 us -> 2.11 us
    pallas_call x1, Pallas kernels: 24.6 us -> 23.5 us  [fused(): pl.pallas_call(functools.partial(fused_kernel, groups, ranks, chains, ami...]
where the time goes in v2:
time: 26.4 us; the launch traced here: 26.2 us
  Pallas kernels  23.5 us (89%)
  local copies, waits for them, and re-layouts  2.11 us (8%)
  between operations  0.65 us (2%)
    pallas_call x1, Pallas kernels, fused(): pl.pallas_call(functools.partial(fused_kernel, groups, ranks, chains, ami...  23.5 us
    unnamed x4, local copies, waits for them, and re-layouts  2.11 us

profile of v2, /device:TPU:0, one launch (start us, length us, event | category | flops | bytes accessed | tf_op | source)
XLA Modules:
  0.0 26.2 jit_solution(5784871733562048038)
XLA Ops:
  0.6 23.5 %shard_map.104 = (bf16[32,4,256]{2,1,0:T(4,128)(2,1)}, bf16[64,128]{1,0:T(8,128)(2,1)}) custom-call(bf16[32,4,256]{2,1,0:T(4,128)(2,1)} %emb_ref.1, s32[4,32]{1,0:T(4,128)} %bitcast.9, s32[1,32]{1,0:T(1,128)} %bitcast.11, bf16[64,128]{1,0:T(8,128)(2,1)} %bitcast.7, bf16[256,1024]{1,0:T(8,128)(2,1)} %proj_ref.1, bf16[8,128]{1,0:T(8,128)(2,1)} %bitcast.10, ...), custom_call_target="tpu_custom_call" | custom-call | tf_op jit(solution)/shard_map/pallas_call | solution.py:431
  24.1 0.0 copy-start
  24.1 1.5 %copy.13 = bf16[32,4,256]{2,1,0:T(4,128)(2,1)} copy(bf16[32,4,256]{2,1,0:T(4,128)(2,1)} %get-tuple-element.8) | data formatting | bytes 131072
  25.6 0.0 copy-done
  25.6 0.6 %copy.14 = bf16[16,4,128]{2,1,0:T(4,128)(2,1)} copy(bf16[16,4,128]{2,1,0:T(4,128)(2,1)S(1)} %bitcast.8) | data formatting | bytes 32768
Async XLA Ops:
  24.1 1.5 %copy-start = (bf16[64,128]{1,0:T(8,128)(2,1)S(1)}, bf16[64,128]{1,0:T(8,128)(2,1)}, u32[]{:S(2)}) copy-start(bf16[64,128]{1,0:T(8,128)(2,1)} %get-tuple-element.5) | copy-start | bytes 49156

commit v3 on v2

--- a/solution.py
+++ b/solution.py
@@ -196,11 +196,11 @@
 
 def fused_kernel(
     groups, ranks, chains, aminos,
-    emb_ref, mask_ref, resolved_ref, pair_ref, proj_ref, bias_w_ref, final_ref, lr_ref, outer_ref,
+    emb_ref, mask_ref, resolved_ref, pair_ref, proj_hbm, bias_w_ref, final_hbm, lr_ref, outer_hbm,
     out_ref, pair_out_ref,
-    emb_buf, aux_buf, left_send, left_buf, right_send, right_buf, out_send, out_buf,
-    product_buf, lhs_buf,
-    emb_s, emb_r, aux_s, aux_r, left_s, left_r, right_s, right_r, out_s, out_r,
+    emb_buf, aux_buf, side_send, side_buf, out_send, out_buf,
+    product_buf, lhs_buf, proj_ref, final_ref, outer_ref,
+    emb_s, emb_r, aux_s, aux_r, side_s, side_r, out_s, out_r, load_s,
 ):
     devices = groups * ranks
     per = chains // ranks
@@ -223,6 +223,13 @@
         pl.semaphore_signal(
             barrier, inc=1, device_id=peer_of(k)[1], device_id_type=pl.DeviceIdType.MESH
         )
+
+    loads = []
+    for k, (src, dst) in enumerate(
+        ((proj_hbm, proj_ref), (final_hbm, final_ref), (outer_hbm, outer_ref))
+    ):
+        loads.append(pltpu.make_async_copy(src, dst, load_s.at[k]))
+        loads[-1].start()
 
     def send(src, dst, ssem, rsem, device):
         copy = pltpu.make_async_remote_copy(
@@ -283,6 +290,7 @@
         copy.wait_recv()
     embedding = emb_buf[...].astype(F32).reshape(rows, ROW_FEATURES)
     normed = layer_normalize(embedding).astype(BF16)
+    loads[0].wait()
     projected = dot(normed, proj_ref[...])
     width = HEAD_NUMBER * PER_HEAD_DIM
     queries = (projected[:, :width] * PER_HEAD_DIM ** (-0.5)).astype(BF16)
@@ -335,6 +343,7 @@
         mixed.append(total)
     attended = jnp.concatenate(mixed, axis=1).astype(BF16)
     gated = (gating * attended.astype(F32)).astype(BF16)
+    loads[1].wait()
     updated = (embedding + dot(gated, final_ref[...])).astype(BF16)
     normed_out = layer_normalize(updated).astype(BF16)
 
@@ -346,25 +355,25 @@
         part = left[g * half:g * half + tile]
         for r in range(1, quads):
             part = part + left[g * half + r * tile:g * half + (r + 1) * tile]
-        left_send[g] = part.astype(BF16)
+        for r in range(ranks):
+            side_send[g * ranks + r, :tile] = part.astype(BF16)
     right = dot(normed_out, right_w, 1, 1) * present
     right = jnp.where(ll // PROJ_FEATURES == pp % aminos, right, 0.0).astype(BF16)
-    right_send[...] = right.reshape(ranks, tile, LANES)
+    for d in range(devices):
+        at = d % ranks * tile
+        side_send[d, tile:] = right[at:at + tile]
     out_send[...] = updated.astype(F32).reshape(chains, aminos, ROW_FEATURES).astype(BF16)
     left_copies = []
     for k in range(1, devices):
         peer, device = peer_of(k)
-        left_copies.append(send(left_send.at[peer // ranks], left_buf.at[me],
-                                left_s.at[k], left_r.at[k], device))
-        left_copies.append(send(right_send.at[lax.rem(peer, ranks)], right_buf.at[me],
-                                right_s.at[k], right_r.at[k], device))
+        left_copies.append(send(side_send.at[peer], side_buf.at[me], side_s.at[k], side_r.at[k],
+                                device))
     out_copies = []
     for k in range(1, ranks):
         peer = lax.rem(rank + k, ranks)
         out_copies.append(send(out_send.at[pl.ds(peer * per, per)], out_buf.at[own], out_s.at[k], out_r.at[k],
                                {"seq": group, "res": peer}))
-    left_buf[me] = left_send[group]
-    right_buf[me] = right_send[rank]
+    side_buf[me] = side_send[me]
     out_buf[own] = out_send[own]
 
     gq = (groups * pairs, devices)
@@ -390,8 +399,8 @@
     block = iota((pair_rows, LANES), 1) // PROJ_FEATURES
     for copy in left_copies:
         copy.wait_recv()
-    left_all = left_buf[...].reshape(depth, LANES)
-    right_all = dot(rep, right_buf[...].reshape(depth, LANES))
+    left_all = side_buf[:, :tile].reshape(depth, LANES)
+    right_all = dot(rep, side_buf[:, tile:].reshape(depth, LANES))
     right_all = jnp.concatenate(
         [jnp.where(amino_d == a, right_all, 0.0).astype(BF16) for a in range(aminos)], axis=1)
     product = dot(left_all, right_all, 0, 0)
@@ -408,6 +417,7 @@
                 turned = jnp.where(block == x, moved, turned)
             lhs_buf[j * pair_rows:(j + 1) * pair_rows,
                     c * PROJ_FEATURES:c * PROJ_FEATURES + LANES] = turned.astype(BF16)
+    loads[2].wait()
     outer = dot(lhs_buf[...], outer_ref[...])
     result = (pair_turned + pair_mask * (outer / counts)).astype(BF16)
     pair_out_ref[...] = dot(order, result, 0, 0).astype(BF16)
@@ -427,6 +437,7 @@
     pair_rows = pair.shape[0]
     devices = groups * ranks
     vmem = pl.BlockSpec(memory_space=pltpu.VMEM)
+    whole = pl.BlockSpec(memory_space=pl.ANY)
     dma = pltpu.SemaphoreType.DMA
     out, pair_out = pl.pallas_call(
         functools.partial(fused_kernel, groups, ranks, chains, aminos),
@@ -434,22 +445,22 @@
             jax.ShapeDtypeStruct(emb.shape, BF16),
             jax.ShapeDtypeStruct((pair_rows * aminos, CZ), BF16),
         ),
-        in_specs=[vmem] * 9,
+        in_specs=[vmem] * 4 + [whole, vmem, whole, vmem, whole],
         out_specs=(vmem, vmem),
         scratch_shapes=[
             pltpu.VMEM(emb.shape, BF16),
             pltpu.VMEM((devices, 2 * HEAD_NUMBER, LANES), BF16),
-            pltpu.VMEM((groups, tile, LANES), BF16),
-            pltpu.VMEM((devices, tile, LANES), BF16),
-            pltpu.VMEM((ranks, tile, LANES), BF16),
-            pltpu.VMEM((devices, tile, LANES), BF16),
+            pltpu.VMEM((devices, 2 * tile, LANES), BF16),
+            pltpu.VMEM((devices, 2 * tile, LANES), BF16),
             pltpu.VMEM(emb.shape, BF16),
             pltpu.VMEM(emb.shape, BF16),
             pltpu.VMEM((pair_rows * PROJ_FEATURES, LANES), F32),
             pltpu.VMEM((pair_rows * aminos, PROJ_FEATURES * PROJ_FEATURES), BF16),
+            pltpu.VMEM(args[4].shape, BF16),
+            pltpu.VMEM(args[6].shape, BF16),
+            pltpu.VMEM(args[8].shape, BF16),
             dma((ranks,)), dma((ranks,)), dma((devices,)), dma((devices,)),
-            dma((devices,)), dma((devices,)), dma((devices,)), dma((devices,)),
-            dma((ranks,)), dma((ranks,)),
+            dma((devices,)), dma((devices,)), dma((ranks,)), dma((ranks,)), dma((3,)),
         ],
         compiler_params=pltpu.CompilerParams(collective_id=0, has_side_effects=True),
     )(

time: 26.4 us -> 25.7 us (0.973)
  Pallas kernels: 23.5 us -> 22.6 us
    pallas_call x1, Pallas kernels: 23.5 us -> 22.6 us  [fused(): pl.pallas_call(functools.partial(fused_kernel, groups, ranks, chains, ami...]
where the time goes in v3:
time: 25.7 us; the launch traced here: 25.3 us
  Pallas kernels  22.6 us (88%)
  local copies, waits for them, and re-layouts  2.11 us (8%)
  between operations  0.65 us (3%)
    pallas_call x1, Pallas kernels, fused(): pl.pallas_call(functools.partial(fused_kernel, groups, ranks, chains, ami...  22.6 us
    unnamed x4, local copies, waits for them, and re-layouts  2.11 us

profile of v3, /device:TPU:0, one launch (start us, length us, event | category | flops | bytes accessed | tf_op | source)
XLA Modules:
  0.0 25.3 jit_solution(11983556159739749718)
XLA Ops:
  0.6 22.6 %shard_map.104 = (bf16[32,4,256]{2,1,0:T(4,128)(2,1)}, bf16[64,128]{1,0:T(8,128)(2,1)}) custom-call(bf16[32,4,256]{2,1,0:T(4,128)(2,1)} %emb_ref.1, s32[4,32]{1,0:T(4,128)} %bitcast.9, s32[1,32]{1,0:T(1,128)} %bitcast.11, bf16[64,128]{1,0:T(8,128)(2,1)} %bitcast.7, bf16[256,1024]{1,0:T(8,128)(2,1)} %proj_hbm.1, bf16[8,128]{1,0:T(8,128)(2,1)} %bitcast.10, ...), custom_call_target="tpu_custom_call" | custom-call | tf_op jit(solution)/shard_map/pallas_call | solution.py:442
  23.2 0.0 copy-start
  23.2 1.5 %copy.13 = bf16[32,4,256]{2,1,0:T(4,128)(2,1)} copy(bf16[32,4,256]{2,1,0:T(4,128)(2,1)} %get-tuple-element.8) | data formatting | bytes 131072
  24.7 0.0 copy-done
  24.7 0.6 %copy.14 = bf16[16,4,128]{2,1,0:T(4,128)(2,1)} copy(bf16[16,4,128]{2,1,0:T(4,128)(2,1)S(1)} %bitcast.8) | data formatting | bytes 32768
Async XLA Ops:
  23.2 1.5 %copy-start = (bf16[64,128]{1,0:T(8,128)(2,1)S(1)}, bf16[64,128]{1,0:T(8,128)(2,1)}, u32[]{:S(2)}) copy-start(bf16[64,128]{1,0:T(8,128)(2,1)} %get-tuple-element.5) | copy-start | bytes 49156
